TPU v7x, 32 devices: a whole 2x2x4 slice. The times are simulated.
32 devices in a mesh: seq: 4 (over x, core), mp: 8 (over z, y).
Axes of the slice: x: 2, y: 2, z: 4, core: 2. Of those that a mesh axis runs over, the one named last changes fastest.
Arguments:
- byte_states: bfloat16 [4, 4096, 1024], P('seq', 'mp'), may hold values from -312 to 312
- patch_latents: bfloat16 [4, 1024, 4096], P(None, 'seq', 'mp'), may hold values from -6 to 6
- patch_lengths: int32 [4, 1024], P('seq'), may hold values from 1 to 12, 4096 in all within a row
- w_down: bfloat16 [4096, 1024], replicated, may hold values from -0.09375 to 0.09375
- kv_gain: bfloat16 [1024], replicated, may hold values from 0.25 to 1.75
- w_query: bfloat16 [1024, 1024], replicated, may hold values from -0.375 to 0.375
- w_key: bfloat16 [1024, 1024], replicated, may hold values from -0.1875 to 0.1875
- w_value: bfloat16 [1024, 1024], replicated, may hold values from -0.1875 to 0.1875
- w_out: bfloat16 [1024, 1024], replicated, may hold values from -0.375 to 0.375
- out_gain: bfloat16 [1024], replicated, may hold values from 0.25 to 1.75
Outputs:
- decoded: bfloat16 [4, 4096, 1024], P('seq', 'mp')
Inputs may be any that keep to these rules, and one draw needn't show every extreme that they name: patch_lengths[s] lists the lengths of the 1024 patches of sequence s in order; they sum to 4096 and the longest is exactly 12.
All inputs are finite; a program needn't handle non-finite values.
Results may differ from a plain program's by a relative error of at most 0.0076.
Values may be sent and summed in bfloat16 or wider, within the bound.
A program may use at most 128 MiB of HBM per device.

v0:
```python
import math

import jax
import jax.numpy as jnp
from jax import lax
from jax.sharding import PartitionSpec as P

HEADS = 16
HEAD_DIM = 64


NEG_FLOOR = -1e30


def rms_norm(values, gain_row):
    mean_square = jnp.mean(values * values, axis=-1, keepdims=True)
    return values * lax.rsqrt(mean_square + 1e-05) * gain_row.astype(jnp.float32)


def fold_block(fold_state, query_part, position_part, key_block, value_block, start_block):
    row_max, denominator, accumulated = fold_state
    scale_factor = 1.0 / math.sqrt(HEAD_DIM)
    scores = (
        jnp.einsum("rhd,khd->hrk", query_part, key_block, preferred_element_type=jnp.float32)
        * scale_factor
    )
    allowed = start_block[None, None, :] <= position_part[None, :, None]
    masked = jnp.where(allowed, scores, NEG_FLOOR)
    new_max = jnp.maximum(row_max, jnp.max(masked, axis=-1))
    raised = jnp.where(allowed, jnp.exp(masked - new_max[..., None]), 0.0)
    correction = jnp.exp(row_max - new_max)
    denominator = denominator * correction + jnp.sum(raised, axis=-1)
    accumulated = accumulated * correction[..., None] + jnp.einsum(
        "hrk,khd->hrd", raised.astype(jnp.bfloat16), value_block, preferred_element_type=jnp.float32
    )
    return (new_max, denominator, accumulated)


def make_folder(query_halves, position_halves, starts):

    def folder(running, arrived_piece, piece_start):
        key_piece, value_piece = arrived_piece
        piece_rows = key_piece.shape[0]
        step_rows = math.gcd(piece_rows, 512)

        def one_block(block_index, fold_state):
            offset = block_index * step_rows
            key_block = lax.dynamic_slice_in_dim(key_piece, offset, step_rows, 0).reshape(
                step_rows, HEADS, HEAD_DIM
            )
            value_block = lax.dynamic_slice_in_dim(value_piece, offset, step_rows, 0).reshape(
                step_rows, HEADS, HEAD_DIM
            )
            start_block = lax.dynamic_slice_in_dim(starts, offset, step_rows, 0)
            updated = []
            for part_index in range(2):
                part_state = tuple((member[part_index] for member in fold_state))

                def advance(inner_state, part_index=part_index):
                    return fold_block(
                        inner_state,
                        query_halves[part_index],
                        position_halves[part_index],
                        key_block,
                        value_block,
                        start_block,
                    )

                def remain(inner_state):
                    return inner_state

                needed = start_block[0] <= position_halves[part_index][-1]
                updated.append(lax.cond(needed, advance, remain, part_state))
            return tuple((jnp.stack([updated[0][slot], updated[1][slot]]) for slot in range(3)))

        return lax.fori_loop(0, piece_rows // step_rows, one_block, running)

    return folder


def per_device(
    byte_states,
    patch_latents,
    patch_lengths,
    w_down,
    kv_gain,
    w_query,
    w_key,
    w_value,
    w_out,
    out_gain,
):
    my_rank = lax.axis_index("mp")
    tokens_here = byte_states.shape[1]
    half_rows = tokens_here // 2
    regrouped = lax.all_to_all(
        lax.all_to_all(patch_latents, "seq", split_axis=0, concat_axis=1, tiled=True),
        "mp",
        split_axis=1,
        concat_axis=2,
        tiled=True,
    )
    projected = jnp.dot(regrouped[0], w_down, preferred_element_type=jnp.float32)
    patch_normed = rms_norm(projected, kv_gain).astype(jnp.bfloat16)
    lengths = patch_lengths[0]
    starts = jnp.cumsum(lengths) - lengths
    own_rows = byte_states[0]
    local_offsets = jnp.arange(half_rows, dtype=jnp.int32)
    first_position = my_rank * tokens_here
    position_halves = jnp.stack(
        [first_position + local_offsets, first_position + half_rows + local_offsets]
    )
    queries = jnp.dot(own_rows, w_query, preferred_element_type=jnp.float32).astype(jnp.bfloat16)
    query_halves = queries.reshape(2, half_rows, HEADS, HEAD_DIM)
    initial = (
        jnp.full((2, HEADS, half_rows), NEG_FLOOR, jnp.float32),
        jnp.zeros((2, HEADS, half_rows), jnp.float32),
        jnp.zeros((2, HEADS, half_rows, HEAD_DIM), jnp.float32),
    )
    key_rows = jnp.dot(patch_normed, w_key, preferred_element_type=jnp.float32).astype(jnp.bfloat16)
    value_rows = jnp.dot(patch_normed, w_value, preferred_element_type=jnp.float32).astype(
        jnp.bfloat16
    )
    folder = make_folder(query_halves, position_halves, starts)
    row_max, denominator, accumulated = folder(
        initial,
        (
            lax.all_gather(key_rows, "mp", axis=0, tiled=True),
            lax.all_gather(value_rows, "mp", axis=0, tiled=True),
        ),
        jnp.int32(0),
    )
    summed = accumulated / denominator[..., None]
    head_out = (
        jnp.transpose(summed, (0, 2, 1, 3))
        .reshape(tokens_here, HEADS * HEAD_DIM)
        .astype(jnp.bfloat16)
    )
    residual = own_rows.astype(jnp.float32) + jnp.dot(
        head_out, w_out, preferred_element_type=jnp.float32
    )
    decoded = rms_norm(residual, out_gain).astype(jnp.bfloat16)
    return decoded[None]


def solution(mesh):
    return jax.shard_map(
        per_device,
        mesh=mesh,
        in_specs=(
            P("seq", "mp", None),
            P(None, "seq", "mp"),
            P("seq", None),
            P(),
            P(),
            P(),
            P(),
            P(),
            P(),
            P(),
        ),
        out_specs=P("seq", "mp", None),
        check_vma=False,
    )
```

profile of v0, /device:TPU:16, one launch (start us, length us, event | category | flops | bytes accessed | tf_op | source)
XLA Modules:
  0.0 283.9 jit_solution(9395675272807082795)
XLA Ops:
  6.5 18.0 %all_to_all.27 = bf16[4,256,512]{2,1,0:T(8,128)(2,1)S(1)} all-to-all(bf16[4,256,512]{2,1,0:T(8,128)(2,1)} %param.17), channel_id=1, replica_groups=mesh['seq'=4,'mp'=8] {'seq'}, dimensions={0} | all-to-all | bytes 2097152 | tf_op jit(solution)/shard_map/all_to_all | solution.py:97
  28.1 8.0 %reduce.2 = bf16[1024,512]{1,0:T(8,128)(2,1)S(1)} reduce(bf16[1024,1,512]{2,1,0:T(2,128)(2,1)} %bitcast.98, bf16[]{:T(256)} %broadcast.104), dimensions={1}, to_apply=%bitcast.78.reduce_sub_computation | reduce | bytes 2097154
  37.7 6.2 %all-to-all-start.1 = ((bf16[8,2,32768]{2,1,0:T(2,128)(2,1)}), bf16[8,2,32768]{2,1,0:T(2,128)(2,1)S(1)}, u32[]{:S(2)}, u32[]{:S(2)}) async-start(bf16[8,2,32768]{2,1,0:T(2,128)(2,1)} %reshape.138), calls=%async_computation.1 | async-start | bytes 2097152 | tf_op jit(solution)/shard_map/all_to_all | solution.py:96
  43.9 22.3 %all-to-all-done.1 = bf16[8,2,32768]{2,1,0:T(2,128)(2,1)S(1)} async-done(((bf16[8,2,32768]{2,1,0:T(2,128)(2,1)}), bf16[8,2,32768]{2,1,0:T(2,128)(2,1)S(1)}, u32[]{:S(2)}, u32[]{:S(2)}) %all-to-all-start.1) | async-done | bytes 1048608 | tf_op jit(solution)/shard_map/all_to_all | solution.py:96
  66.1 3.4 %reshape.139 = bf16[1024,1,512]{2,1,0:T(2,128)(2,1)} reshape(bf16[8,2,32768]{2,1,0:T(2,128)(2,1)S(1)} %all-to-all-done.1) | data formatting | bytes 2097152
  74.0 4.9 %multiply_reduce_fusion.1 = (f32[128]{0:T(128)S(1)}, f32[128,1024]{1,0:T(8,128)S(1)}) fusion(bf16[128,4096]{0,1:T(8,128)(2,1)S(1)} %bitcast.99, bf16[4096,1024]{1,0:T(8,128)(2,1)} %param.19), kind=kOutput, calls=%fused_computation.58 | convolution fusion | flops 1074003840 | bytes 9961984 | tf_op jit(solution)/shard_map/dot_general | solution.py:103
  84.6 3.2 %convolution_convert_fusion = bf16[512,1024]{1,0:T(8,128)(2,1)S(1)} fusion(bf16[1024,1024]{1,0:T(8,128)(2,1)} %param.21, bf16[1,512,1024]{2,1,0:T(8,128)(2,1)} %param.16), kind=kOutput, calls=%fused_computation.51 | convolution fusion | flops 1074266112 | bytes 4194304 | tf_op jit(solution)/shard_map/dot_general | solution.py:113
  90.1 3.6 %copy.36 = bf16[2,256,16,64]{1,3,2,0:T(8,128)(2,1)} copy(bf16[2,256,16,64]{3,2,1,0:T(8,128)(2,1)} %reshape.136) | data formatting | bytes 2097152 | tf_op jit(solution)/shard_map/while | solution.py:76
  93.8 36.8 %all-gather.3.cloned.1.call-done = bf16[1024,1024]{1,0:T(8,128)(2,1)} async-done(((bf16[128,1024]{1,0:T(8,128)(2,1)}), bf16[1024,1024]{1,0:T(8,128)(2,1)}) %all-gather.3.cloned.1.call-update) | async-done | bytes 2097168 | tf_op jit(solution)/shard_map/all_gather | solution.py:128
  130.6 49.8 %all-gather.5.cloned.1.call-done = bf16[1024,1024]{1,0:T(8,128)(2,1)} async-done(((bf16[128,1024]{1,0:T(8,128)(2,1)}), bf16[1024,1024]{1,0:T(8,128)(2,1)}) %all-gather.5.cloned.1.call-update) | async-done | bytes 2097168 | tf_op jit(solution)/shard_map/all_gather | solution.py:129
  182.0 88.0 %while.17 = (s32[]{:T(128)}, f32[2,16,256]{2,1,0:T(8,128)S(1)}, f32[2,16,256]{2,1,0:T(8,128)S(1)}, f32[2,16,256,64]{2,3,1,0:T(8,128)}, s32[1024]{0:T(1024)S(1)},...) while((s32[]{:T(128)}, f32[2,16,256]{2,1,0:T(8,128)S(1)}, ...), condition=%wide.region_12.13_spmd, body=%wide.region_3.12_spmd.sunk | while | flops 1130135552 | bytes 103557752 | solution.py:76
  185.2 3.1 %slice_bitcast_fusion.9 = (f32[16,256,64]{1,2,0:T(8,128)}, f32[16,256,64]{1,2,0:T(8,128)}) fusion(f32[2,16,256,64]{2,3,1,0:T(8,128)} %get-tuple-element.503), kind=kLoop, calls=%fused_computation.38.clone.1 | loop fusion | bytes 4194304 | tf_op jit(solution)/shard_map/while/body/eval_jaxpr/squeeze | solution.py:57
  195.8 11.8 %conditional.4 = (f32[1,16,256]{2,1,0:T(8,128)}, f32[1,16,256]{2,1,0:T(8,128)S(1)}, f32[1,16,256,64]{2,3,1,0:T(8,128)}) conditional(s32[]{:T(128)} %bitcast.87, (f32[16,256]{1,0:T(8,128)}, f32[16,256]{1,0:T(8,128)S(1)}, f32[16,256,64]{1,2,0:T(8,128)}) %tuple.129, (s32[512]{0:T(512)S(1)}, s32[256]{0:T(256)S(1)}, bf16[2,256,16,64]{1,3,2,0:T(8,128)(2,1)}, ...), branch_computations={%region_8.8_spmd, %region_9.0_spmd} | conditional | flops 564797440 | bytes 43224172 | solution.py:73
  199.5 3.2 %fusion.20 = f32[16,256]{1,0:T(8,128)S(1)} fusion(f32[16,256,512]{2,1,0:T(8,128)S(1)} %get-tuple-element.368, f32[16,256]{1,0:T(8,128)} %max.5, pred[256,512]{1,0:T(8,128)(4,1)S(1)} %broadcast_compare_fusion.1), kind=kLoop, calls=%fused_computation.22 | loop fusion | flops 10481664 | bytes 8552448 | tf_op jit(solution)/shard_map/while/body/eval_jaxpr/cond/branch_1_fun/reduce_sum | solution.py:32
  203.5 3.1 %fusion.27 = f32[1,16,256,64]{2,3,1,0:T(8,128)S(1)} fusion(bf16[512,16,64]{0,2,1:T(8,128)(2,1)S(1)} %copy-done.5, f32[16,256,512]{2,1,0:T(8,128)S(1)} %get-tuple-element.368, f32[16,256]{1,0:T(8,128)} %max.5, pred[256,512]{1,0:T(8,128)(4,1)S(1)} %broadcast_compare_fusion.1, f32[16,256,64]{1,2,0:T(8,128)S(1)} %copy-done.3, f32[16,256]{1,0:T(8,128)S(1)} %get-tuple-element.364), kind=kOutput, calls=%fused_computation.26 | convolution fusion | flops 279445504 | bytes 11698176 | tf_op jit(solution)/shard_map/while/body/eval_jaxpr/cond/branch_1_fun/hrk,khd->hrd/dot_general | solution.py:33
  210.3 11.8 %conditional.5 = (f32[1,16,256]{2,1,0:T(8,128)}, f32[1,16,256]{2,1,0:T(8,128)S(1)}, f32[1,16,256,64]{2,3,1,0:T(8,128)}) conditional(s32[]{:T(128)} %bitcast.90, (f32[16,256]{1,0:T(8,128)}, f32[16,256]{1,0:T(8,128)S(1)}, f32[16,256,64]{1,2,0:T(8,128)}) %tuple.131, (s32[512]{0:T(512)S(1)}, s32[256]{0:T(256)S(1)}, bf16[2,256,16,64]{1,3,2,0:T(8,128)(2,1)}, ...), branch_computations={%region_4.4_spmd, %region_5.0_spmd} | conditional | flops 564797440 | bytes 43224172 | solution.py:73
  214.0 3.2 %fusion.2 = f32[16,256]{1,0:T(8,128)S(1)} fusion(f32[16,256,512]{2,1,0:T(8,128)S(1)} %get-tuple-element.366, f32[16,256]{1,0:T(8,128)} %max.4, pred[256,512]{1,0:T(8,128)(4,1)S(1)} %broadcast_compare_fusion), kind=kLoop, calls=%fused_computation.4 | loop fusion | flops 10481664 | bytes 8552448 | tf_op jit(solution)/shard_map/while/body/eval_jaxpr/cond/branch_1_fun/reduce_sum | solution.py:32
  218.0 3.1 %fusion.9 = f32[1,16,256,64]{2,3,1,0:T(8,128)S(1)} fusion(bf16[512,16,64]{0,2,1:T(8,128)(2,1)S(1)} %copy-done.6, f32[16,256,512]{2,1,0:T(8,128)S(1)} %get-tuple-element.366, f32[16,256]{1,0:T(8,128)} %max.4, pred[256,512]{1,0:T(8,128)(4,1)S(1)} %broadcast_compare_fusion, f32[16,256,64]{1,2,0:T(8,128)S(1)} %copy-done.1, f32[16,256]{1,0:T(8,128)S(1)} %get-tuple-element.362), kind=kOutput, calls=%fused_computation.8 | convolution fusion | flops 279445504 | bytes 11698176 | tf_op jit(solution)/shard_map/while/body/eval_jaxpr/cond/branch_1_fun/hrk,khd->hrd/dot_general | solution.py:33
  239.8 11.8 %conditional.4 = (f32[1,16,256]{2,1,0:T(8,128)}, f32[1,16,256]{2,1,0:T(8,128)S(1)}, f32[1,16,256,64]{2,3,1,0:T(8,128)}) conditional(s32[]{:T(128)} %bitcast.87, (f32[16,256]{1,0:T(8,128)}, f32[16,256]{1,0:T(8,128)S(1)}, f32[16,256,64]{1,2,0:T(8,128)}) %tuple.129, (s32[512]{0:T(512)S(1)}, s32[256]{0:T(256)S(1)}, bf16[2,256,16,64]{1,3,2,0:T(8,128)(2,1)}, ...), branch_computations={%region_8.8_spmd, %region_9.0_spmd} | conditional | flops 564797440 | bytes 43224172 | solution.py:73
  243.5 3.2 %fusion.20 = f32[16,256]{1,0:T(8,128)S(1)} fusion(f32[16,256,512]{2,1,0:T(8,128)S(1)} %get-tuple-element.368, f32[16,256]{1,0:T(8,128)} %max.5, pred[256,512]{1,0:T(8,128)(4,1)S(1)} %broadcast_compare_fusion.1), kind=kLoop, calls=%fused_computation.22 | loop fusion | flops 10481664 | bytes 8552448 | tf_op jit(solution)/shard_map/while/body/eval_jaxpr/cond/branch_1_fun/reduce_sum | solution.py:32
  247.5 3.1 %fusion.27 = f32[1,16,256,64]{2,3,1,0:T(8,128)S(1)} fusion(bf16[512,16,64]{0,2,1:T(8,128)(2,1)S(1)} %copy-done.5, f32[16,256,512]{2,1,0:T(8,128)S(1)} %get-tuple-element.368, f32[16,256]{1,0:T(8,128)} %max.5, pred[256,512]{1,0:T(8,128)(4,1)S(1)} %broadcast_compare_fusion.1, f32[16,256,64]{1,2,0:T(8,128)S(1)} %copy-done.3, f32[16,256]{1,0:T(8,128)S(1)} %get-tuple-element.364), kind=kOutput, calls=%fused_computation.26 | convolution fusion | flops 279445504 | bytes 11698176 | tf_op jit(solution)/shard_map/while/body/eval_jaxpr/cond/branch_1_fun/hrk,khd->hrd/dot_general | solution.py:33
  254.3 11.8 %conditional.5 = (f32[1,16,256]{2,1,0:T(8,128)}, f32[1,16,256]{2,1,0:T(8,128)S(1)}, f32[1,16,256,64]{2,3,1,0:T(8,128)}) conditional(s32[]{:T(128)} %bitcast.90, (f32[16,256]{1,0:T(8,128)}, f32[16,256]{1,0:T(8,128)S(1)}, f32[16,256,64]{1,2,0:T(8,128)}) %tuple.131, (s32[512]{0:T(512)S(1)}, s32[256]{0:T(256)S(1)}, bf16[2,256,16,64]{1,3,2,0:T(8,128)(2,1)}, ...), branch_computations={%region_4.4_spmd, %region_5.0_spmd} | conditional | flops 564797440 | bytes 43224172 | solution.py:73
  258.0 3.2 %fusion.2 = f32[16,256]{1,0:T(8,128)S(1)} fusion(f32[16,256,512]{2,1,0:T(8,128)S(1)} %get-tuple-element.366, f32[16,256]{1,0:T(8,128)} %max.4, pred[256,512]{1,0:T(8,128)(4,1)S(1)} %broadcast_compare_fusion), kind=kLoop, calls=%fused_computation.4 | loop fusion | flops 10481664 | bytes 8552448 | tf_op jit(solution)/shard_map/while/body/eval_jaxpr/cond/branch_1_fun/reduce_sum | solution.py:32
  262.0 3.1 %fusion.9 = f32[1,16,256,64]{2,3,1,0:T(8,128)S(1)} fusion(bf16[512,16,64]{0,2,1:T(8,128)(2,1)S(1)} %copy-done.6, f32[16,256,512]{2,1,0:T(8,128)S(1)} %get-tuple-element.366, f32[16,256]{1,0:T(8,128)} %max.4, pred[256,512]{1,0:T(8,128)(4,1)S(1)} %broadcast_compare_fusion, f32[16,256,64]{1,2,0:T(8,128)S(1)} %copy-done.1, f32[16,256]{1,0:T(8,128)S(1)} %get-tuple-element.362), kind=kOutput, calls=%fused_computation.8 | convolution fusion | flops 279445504 | bytes 11698176 | tf_op jit(solution)/shard_map/while/body/eval_jaxpr/cond/branch_1_fun/hrk,khd->hrd/dot_general | solution.py:33
  (109 shorter events, 80.1 us)
Async XLA Ops:
  6.5 266.6 %copy-start = (bf16[1024,1024]{1,0:T(8,128)(2,1)S(1)}, bf16[1024,1024]{1,0:T(8,128)(2,1)}, u32[]{:S(2)}) copy-start(bf16[1024,1024]{1,0:T(8,128)(2,1)} %param.24) | copy-start | bytes 6291460
  6.5 37.3 %copy-start.10 = (bf16[1024]{0:T(1024)(128)(2,1)S(1)}, bf16[1024]{0:T(1024)(128)(2,1)}, u32[]{:S(2)}) copy-start(bf16[1024]{0:T(1024)(128)(2,1)} %param.20) | copy-start | bytes 6148
  37.7 28.5 %all-to-all-start.1 = ((bf16[8,2,32768]{2,1,0:T(2,128)(2,1)}), bf16[8,2,32768]{2,1,0:T(2,128)(2,1)S(1)}, u32[]{:S(2)}, u32[]{:S(2)}) async-start(bf16[8,2,32768]{2,1,0:T(2,128)(2,1)} %reshape.138), calls=%async_computation.1 | async-start | bytes 2097152 | tf_op jit(solution)/shard_map/all_to_all | solution.py:96
  43.9 86.8 %all-gather.3.cloned.1.call-start = ((), (), s32[]{:S(2)}) async-start(), calls=%async_computation.2 | async-start | bytes 2359296 | tf_op jit(solution)/shard_map/all_gather | solution.py:128
  74.0 5.7 %copy-start.8 = (bf16[1024,1024]{1,0:T(8,128)(2,1)S(1)}, bf16[1024,1024]{1,0:T(8,128)(2,1)}, u32[]{:S(2)}) copy-start(bf16[1024,1024]{1,0:T(8,128)(2,1)} %param.22) | copy-start | bytes 6291460
  74.0 10.1 %copy-start.9 = (s32[1,1024]{1,0:T(1,128)S(1)}, s32[1,1024]{1,0:T(1,128)}, u32[]{:S(2)}) copy-start(s32[1,1024]{1,0:T(1,128)} %param.18) | copy-start | bytes 12292
  78.9 0.8 copy-start.7
  80.9 12.7 %copy-start.11 = (bf16[1024]{0:T(1024)(128)(2,1)S(1)}, bf16[1024]{0:T(1024)(128)(2,1)}, u32[]{:S(2)}) copy-start(bf16[1024]{0:T(1024)(128)(2,1)} %param.25) | copy-start | bytes 6148
  80.9 99.5 %all-gather.5.cloned.1.call-start = ((), (), s32[]{:S(2)}) async-start(), calls=%async_computation.3 | async-start | bytes 2359296 | tf_op jit(solution)/shard_map/all_gather | solution.py:129
  195.9 7.5 %copy-start.3 = (f32[16,256,64]{1,2,0:T(8,128)S(1)}, f32[16,256,64]{1,2,0:T(8,128)}, u32[]{:S(2)}) copy-start(f32[16,256,64]{1,2,0:T(8,128)} %get-tuple-element.256) | copy-start | bytes 3145732 | tf_op jit(solution)/shard_map/while/body/eval_jaxpr/cond
  196.0 7.5 %copy-start.5 = (bf16[512,16,64]{0,2,1:T(8,128)(2,1)S(1)}, bf16[512,16,64]{0,2,1:T(8,128)(2,1)}, u32[]{:S(2)}) copy-start(bf16[512,16,64]{0,2,1:T(8,128)(2,1)} %get-tuple-element.257) | copy-start | bytes 3145732 | tf_op jit(solution)/shard_map/while/body/eval_jaxpr/cond
  206.6 1.0 copy-start.4
  210.5 7.5 %copy-start.1 = (f32[16,256,64]{1,2,0:T(8,128)S(1)}, f32[16,256,64]{1,2,0:T(8,128)}, u32[]{:S(2)}) copy-start(f32[16,256,64]{1,2,0:T(8,128)} %get-tuple-element.248) | copy-start | bytes 3145732 | tf_op jit(solution)/shard_map/while/body/eval_jaxpr/cond
  210.5 7.5 %copy-start.6 = (bf16[512,16,64]{0,2,1:T(8,128)(2,1)S(1)}, bf16[512,16,64]{0,2,1:T(8,128)(2,1)}, u32[]{:S(2)}) copy-start(bf16[512,16,64]{0,2,1:T(8,128)(2,1)} %get-tuple-element.249) | copy-start | bytes 3145732 | tf_op jit(solution)/shard_map/while/body/eval_jaxpr/cond
  221.2 1.0 copy-start.2
  240.0 7.5 %copy-start.3 = (f32[16,256,64]{1,2,0:T(8,128)S(1)}, f32[16,256,64]{1,2,0:T(8,128)}, u32[]{:S(2)}) copy-start(f32[16,256,64]{1,2,0:T(8,128)} %get-tuple-element.256) | copy-start | bytes 3145732 | tf_op jit(solution)/shard_map/while/body/eval_jaxpr/cond
  240.0 7.5 %copy-start.5 = (bf16[512,16,64]{0,2,1:T(8,128)(2,1)S(1)}, bf16[512,16,64]{0,2,1:T(8,128)(2,1)}, u32[]{:S(2)}) copy-start(bf16[512,16,64]{0,2,1:T(8,128)(2,1)} %get-tuple-element.257) | copy-start | bytes 3145732 | tf_op jit(solution)/shard_map/while/body/eval_jaxpr/cond
  250.7 1.0 copy-start.4
  254.5 7.5 %copy-start.1 = (f32[16,256,64]{1,2,0:T(8,128)S(1)}, f32[16,256,64]{1,2,0:T(8,128)}, u32[]{:S(2)}) copy-start(f32[16,256,64]{1,2,0:T(8,128)} %get-tuple-element.248) | copy-start | bytes 3145732 | tf_op jit(solution)/shard_map/while/body/eval_jaxpr/cond
  254.5 7.5 %copy-start.6 = (bf16[512,16,64]{0,2,1:T(8,128)(2,1)S(1)}, bf16[512,16,64]{0,2,1:T(8,128)(2,1)}, u32[]{:S(2)}) copy-start(bf16[512,16,64]{0,2,1:T(8,128)(2,1)} %get-tuple-element.249) | copy-start | bytes 3145732 | tf_op jit(solution)/shard_map/while/body/eval_jaxpr/cond
  265.2 1.0 copy-start.2
Sparse Core Ops, SparseCore 0:
  81.1 49.5 all-gather.2
  132.7 47.6 all-gather.4
where the time goes:
time: 286 us; the launch traced here: 284 us
  waiting for transfers between devices  109 us (38%)
  local copies, waits for them, and re-layouts  54.5 us (19%)
  matrix products  39.1 us (14%)
  other arithmetic  38 us (13%)
  blocking collectives  18 us (6%)
  between operations  13.5 us (5%)
  starting transfers between devices  6.39 us (2%)
  loops' own time  5.51 us (2%)
    all_gather x1, waiting for transfers between devices, per_device(): lax.all_gather(value_rows, 'mp', axis=0, tiled=True)  49.8 us
    all_gather x1, waiting for transfers between devices, per_device(): lax.all_gather(key_rows, 'mp', axis=0, tiled=True)  36.8 us
    all_to_all x1, waiting for transfers between devices, per_device(): lax.all_to_all(lax.all_to_all(patch_latents, 'seq', split_axis=0, concat_...  22.3 us
    all_to_all x1, blocking collectives, per_device(): lax.all_to_all(patch_latents, 'seq', split_axis=0, concat_axis=1, tiled=T...  18 us
    reduce_sum x4, other arithmetic, fold_block(): denominator = denominator * correction + jnp.sum(raised, axis=-1)  12.9 us
    dot_general x4, matrix products, fold_block(): jnp.einsum('hrk,khd->hrd', raised.astype(jnp.bfloat16), value_block, pref...  12.6 us
    dot_general x4, matrix products, fold_block(): jnp.einsum('rhd,khd->hrk', query_part, key_block, preferred_element_type=...  11.7 us
    another operation x10, other arithmetic, one_block(): jnp.stack([updated[0][slot], updated[1][slot]])  10.6 us
  transfers between devices with their start and end apart: 3, of which 3 were waited for; matrix products, arithmetic and copies ran while one was open for 4% of the time, Pallas kernels for 0%

commit v1 on v0

v1 whole, which is shorter than its diff:
```python
import functools

import jax
import jax.numpy as jnp
from jax import lax
from jax.experimental import pallas as pl
from jax.experimental.pallas import tpu as pltpu
from jax.sharding import PartitionSpec as P

HEADS = 16
HEAD_DIM = 64
MASKED = -1e30
MESH = pl.DeviceIdType.MESH


def rms_norm(values, gain_row):
    mean_square = jnp.mean(values * values, axis=-1, keepdims=True)
    return values * lax.rsqrt(mean_square + 1e-05) * gain_row


def exchange_kernel(
    n_seq, n_mp, inner,
    lat, wd, gain, bs, wq, wk, wv,
    q_out, k_out, v_out,
    latbuf, gbuf, acc, wd_v, bs_v, wq_v, wk_v, wv_v,
    load_sem, send_sem, recv_sem, up_sem, down_sem, pair_sem, got_sem,
):
    my_s = lax.axis_index("seq")
    my_m = lax.axis_index("mp")
    total = n_seq * n_mp
    me = my_s * n_mp + my_m
    piece = lat.shape[1] // n_mp
    feats = lat.shape[2]
    width = acc.shape[1]
    tile = 256

    loads = [
        pltpu.make_async_copy(src, dst, load_sem.at[i])
        for i, (src, dst) in enumerate(
            [(bs, bs_v), (wq, wq_v), (wd, wd_v), (wk, wk_v), (wv, wv_v)]
        )
    ]
    for load in loads:
        load.start()

    barrier = pltpu.get_barrier_semaphore()

    def greet(step, carry):
        other = lax.rem(me + step, total)
        pl.semaphore_signal(
            barrier, inc=1,
            device_id={"seq": other // n_mp, "mp": lax.rem(other, n_mp)},
            device_id_type=MESH,
        )
        return carry

    lax.fori_loop(1, total, greet, 0)
    pl.semaphore_wait(barrier, total - 1)

    def piece_copy(other):
        t, m = other // n_mp, lax.rem(other, n_mp)
        return pltpu.make_async_remote_copy(
            src_ref=lat.at[t, pl.ds(pl.multiple_of(m * piece, piece), piece), :],
            dst_ref=latbuf.at[my_m, pl.ds(pl.multiple_of(my_s * piece, piece), piece), :],
            send_sem=send_sem.at[other],
            recv_sem=recv_sem.at[me],
            device_id={"seq": t, "mp": m},
            device_id_type=MESH,
        )

    def piece_arrival(s, m):
        here = latbuf.at[m, pl.ds(pl.multiple_of(s * piece, piece), piece), :]
        return pltpu.make_async_copy(here, here, recv_sem.at[s * n_mp + m])

    def send_piece(step, carry):
        piece_copy(lax.rem(me + step, total)).start()
        return carry

    lax.fori_loop(1, total, send_piece, 0)
    pltpu.make_async_copy(
        lat.at[my_s, pl.ds(pl.multiple_of(my_m * piece, piece), piece), :],
        latbuf.at[my_m, pl.ds(pl.multiple_of(my_s * piece, piece), piece), :],
        recv_sem.at[me],
    ).start()

    loads[0].wait()
    loads[1].wait()

    def query_tile(j, carry):
        cols = pl.ds(pl.multiple_of(j * tile, tile), tile)
        made = jnp.dot(bs_v[...], wq_v[:, cols], preferred_element_type=jnp.float32)
        q_out[:, cols] = made.astype(jnp.bfloat16) * jnp.bfloat16(HEAD_DIM**-0.5)
        return carry

    lax.fori_loop(0, wq_v.shape[1] // tile, query_tile, 0)

    loads[2].wait()
    acc[...] = jnp.zeros_like(acc)

    def project(step, carry):
        m = lax.rem(my_m + step, n_mp)

        def arrived(s, inner_carry):
            piece_arrival(s, m).wait()
            return inner_carry

        lax.fori_loop(0, n_seq, arrived, 0)
        rows = pl.ds(pl.multiple_of(m * feats, feats), feats)
        acc[...] += jnp.dot(latbuf[m], wd_v[rows, :], preferred_element_type=jnp.float32)
        return carry

    lax.fori_loop(0, n_mp, project, 0)
    gbuf[my_m] = rms_norm(acc[...], gain[...].astype(jnp.float32)).astype(jnp.bfloat16)

    outer = n_mp // inner
    my_o = my_m // inner
    my_i = lax.rem(my_m, inner)
    partner = my_o * inner + (inner - 1 - my_i)

    def row_copy(chunk, sem, target):
        return pltpu.make_async_remote_copy(
            src_ref=gbuf.at[chunk],
            dst_ref=gbuf.at[chunk],
            send_sem=sem.at[chunk],
            recv_sem=got_sem.at[chunk],
            device_id={"seq": my_s, "mp": target},
            device_id_type=MESH,
        )

    def wait_chunk(chunk):
        pltpu.make_async_copy(gbuf.at[chunk], gbuf.at[chunk], got_sem.at[chunk]).wait()

    def go_up(chunk):
        return row_copy(chunk, up_sem, my_m + inner)

    def go_down(chunk):
        return row_copy(chunk, down_sem, my_m - inner)

    def go_pair(chunk):
        return row_copy(chunk, pair_sem, partner)

    has_up = my_o < outer - 1
    has_down = my_o > 0
    pl.when(has_up)(lambda: go_up(my_m).start())
    pl.when(has_down)(lambda: go_down(my_m).start())
    go_pair(my_m).start()

    def relay(k, carry):
        below = my_m - k * inner
        above = my_m + k * inner

        @pl.when(my_o - k >= 0)
        def _():
            wait_chunk(below)
            pl.when(has_up)(lambda: go_up(below).start())
            go_pair(below).start()

        @pl.when(my_o + k < outer)
        def _():
            wait_chunk(above)
            pl.when(has_down)(lambda: go_down(above).start())
            go_pair(above).start()

        return carry

    lax.fori_loop(1, outer, relay, 0)

    def take_pair(o, carry):
        wait_chunk(o * inner + (inner - 1 - my_i))
        return carry

    lax.fori_loop(0, outer, take_pair, 0)
    loads[3].wait()
    loads[4].wait()

    def kv_tile(j, carry):
        cols = pl.ds(pl.multiple_of(j * tile, tile), tile)
        for c in range(n_mp // 8):
            normed = gbuf[pl.ds(c * 8, 8)].reshape(8 * gbuf.shape[1], width)
            rows = pl.ds(c * 8 * gbuf.shape[1], 8 * gbuf.shape[1])
            k_out[rows, cols] = jnp.dot(
                normed, wk_v[:, cols], preferred_element_type=jnp.float32
            ).astype(jnp.bfloat16)
            v_out[rows, cols] = jnp.dot(
                normed, wv_v[:, cols], preferred_element_type=jnp.float32
            ).astype(jnp.bfloat16)
        return carry

    lax.fori_loop(0, wk_v.shape[1] // tile, kv_tile, 0)

    def finish_piece(step, carry):
        piece_copy(lax.rem(me + step, total)).wait_send()
        return carry

    lax.fori_loop(1, total, finish_piece, 0)

    def finish_rows(o, carry):
        chunk = o * inner + my_i
        pl.when(has_up & (o <= my_o))(lambda: go_up(chunk).wait_send())
        pl.when(has_down & (o >= my_o))(lambda: go_down(chunk).wait_send())
        go_pair(chunk).wait_send()
        return carry

    lax.fori_loop(0, outer, finish_rows, 0)


def attend_kernel(
    rows, q, k, v, starts, positions, bs, w_out, out_gain, out, bias, v_ext, head_out
):
    pair = pl.program_id(0)
    tokens = bias.shape[0]
    lanes = q.shape[1]

    @pl.when(pair == 0)
    def _():
        bias[...] = jnp.where(starts[...] <= positions[...], 0.0, MASKED)
        v_ext[:, lanes:] = jnp.ones((v_ext.shape[0], lanes), v_ext.dtype)

    v_ext[:, :lanes] = v[...]
    lane = lax.broadcasted_iota(jnp.int32, (rows, lanes), 1)
    low = lane < HEAD_DIM

    def one_block(b, carry):
        at = pl.ds(pl.multiple_of(b * rows, rows), rows)
        both = q[at, :]
        parts = []
        for half in range(2):
            keep = low if half == 0 else ~low
            q_half = jnp.where(keep, both, jnp.zeros_like(both))
            scores = lax.dot_general(
                q_half, k[...], (((1,), (1,)), ((), ())), preferred_element_type=jnp.float32
            ) + bias[at, :]
            weights = jnp.exp(scores - jnp.max(scores, axis=-1, keepdims=True))
            summed = jnp.dot(
                weights.astype(jnp.bfloat16), v_ext[...], preferred_element_type=jnp.float32
            )
            parts.append(summed[:, :lanes] / summed[:, lanes:])
        head_out[pair, at, :] = jnp.where(low, parts[0], parts[1]).astype(jnp.bfloat16)
        return carry

    blocks = tokens // rows
    lax.fori_loop(0, blocks, one_block, 0, unroll=blocks <= 2)

    @pl.when(pair == pl.num_programs(0) - 1)
    def _():
        joined = jnp.concatenate([head_out[p] for p in range(head_out.shape[0])], axis=1)
        residual = bs[...].astype(jnp.float32) + jnp.dot(
            joined, w_out[...], preferred_element_type=jnp.float32
        )
        out[...] = rms_norm(residual, out_gain[...].astype(jnp.float32)).astype(out.dtype)


def per_device(n_seq, n_mp, byte_states, patch_latents, patch_lengths, w_down, kv_gain,
               w_query, w_key, w_value, w_out, out_gain):
    own_rows = byte_states[0]
    tokens, width = own_rows.shape
    patches = patch_lengths.shape[1]
    here = patches // n_mp
    feats = patch_latents.shape[2]
    inner = 2
    any_spec = pl.BlockSpec(memory_space=pl.ANY)
    vmem_spec = pl.BlockSpec(memory_space=pltpu.VMEM)
    bf16 = jnp.bfloat16
    queries, key_rows, value_rows = pl.pallas_call(
        functools.partial(exchange_kernel, n_seq, n_mp, inner),
        name="exchange",
        out_shape=(
            jax.ShapeDtypeStruct((tokens, width), bf16),
            jax.ShapeDtypeStruct((patches, width), bf16),
            jax.ShapeDtypeStruct((patches, width), bf16),
        ),
        in_specs=[any_spec, any_spec, vmem_spec] + [any_spec] * 4,
        out_specs=(vmem_spec,) * 3,
        scratch_shapes=[
            pltpu.VMEM((n_mp, here, feats), bf16),
            pltpu.VMEM((n_mp, here, width), bf16),
            pltpu.VMEM((here, width), jnp.float32),
            pltpu.VMEM(w_down.shape, bf16),
            pltpu.VMEM((tokens, width), bf16),
            pltpu.VMEM(w_query.shape, bf16),
            pltpu.VMEM(w_key.shape, bf16),
            pltpu.VMEM(w_value.shape, bf16),
            pltpu.SemaphoreType.DMA((5,)),
            pltpu.SemaphoreType.DMA((n_seq * n_mp,)),
            pltpu.SemaphoreType.DMA((n_seq * n_mp,)),
            pltpu.SemaphoreType.DMA((n_mp,)),
            pltpu.SemaphoreType.DMA((n_mp,)),
            pltpu.SemaphoreType.DMA((n_mp,)),
            pltpu.SemaphoreType.DMA((n_mp,)),
        ],
        compiler_params=pltpu.CompilerParams(
            collective_id=0, has_side_effects=True, vmem_limit_bytes=60 * 1024 * 1024
        ),
    )(patch_latents, w_down, kv_gain[None], own_rows, w_query, w_key, w_value)

    lengths = patch_lengths[0]
    starts = jnp.cumsum(lengths) - lengths
    starts = starts.reshape(n_seq, n_mp, here // n_seq).transpose(1, 0, 2).reshape(1, patches)
    positions = (
        lax.axis_index("mp") * tokens + lax.broadcasted_iota(jnp.int32, (tokens, 1), 0)
    )
    lanes = 2 * HEAD_DIM
    rows = max(16, min(256, (256 * 1024) // patches))
    whole = lambda shape: pl.BlockSpec(shape, lambda p: (0, 0))
    decoded = pl.pallas_call(
        functools.partial(attend_kernel, rows),
        name="attend",
        grid=(width // lanes,),
        out_shape=jax.ShapeDtypeStruct((tokens, width), bf16),
        in_specs=[
            pl.BlockSpec((tokens, lanes), lambda p: (0, p)),
            pl.BlockSpec((patches, lanes), lambda p: (0, p)),
            pl.BlockSpec((patches, lanes), lambda p: (0, p)),
            whole((1, patches)),
            whole((tokens, 1)),
            whole((tokens, width)),
            whole((width, width)),
            whole((1, width)),
        ],
        out_specs=whole((tokens, width)),
        scratch_shapes=[
            pltpu.VMEM((tokens, patches), jnp.float32),
            pltpu.VMEM((patches, 2 * lanes), bf16),
            pltpu.VMEM((width // lanes, tokens, lanes), bf16),
        ],
        compiler_params=pltpu.CompilerParams(
            dimension_semantics=("arbitrary",), vmem_limit_bytes=60 * 1024 * 1024
        ),
    )(queries, key_rows, value_rows, starts, positions, own_rows, w_out, out_gain[None])
    return decoded[None]


def solution(mesh):
    return jax.shard_map(
        functools.partial(per_device, mesh.shape["seq"], mesh.shape["mp"]),
        mesh=mesh,
        in_specs=(
            P("seq", "mp", None),
            P(None, "seq", "mp"),
            P("seq", None),
            P(), P(), P(), P(), P(), P(), P(),
        ),
        out_specs=P("seq", "mp", None),
        check_vma=False,
    )
```

time: 286 us -> 97 us (0.34)
  the two profiles are of different devices: /device:TPU:16 before, /device:TPU:0 now
where the time goes in v1:
time: 97 us; the launch traced here: 96.7 us
  Pallas kernels  89.2 us (92%)
  local copies, waits for them, and re-layouts  4.33 us (4%)
  other arithmetic  3.14 us (3%)
    pallas_call x1, Pallas kernels, per_device(): pl.pallas_call(functools.partial(exchange_kernel, n_seq, n_mp, inner), na...  69.2 us
    pallas_call x1, Pallas kernels, per_device(): pl.pallas_call(functools.partial(attend_kernel, rows), name='attend', gri...  20 us

profile of v1, /device:TPU:0, one launch (start us, length us, event | category | flops | bytes accessed | tf_op | source)
XLA Modules:
  0.0 96.7 jit_solution(2050701528356896357)
XLA Ops:
  0.0 0.5 broadcast.23
  0.5 1.3 %reduce.5 = s32[1024]{0:T(1024)S(1)} reduce(s32[1,1024]{1,0:T(1,128)} %param.12, s32[]{:T(128)} %broadcast.23), dimensions={0}, to_apply=%param.12.reduce_sub_computation.3 | reduce | bytes 8196 | tf_op args[2]
  1.9 1.0 %reduce-window.9 = s32[8,128]{1,0:T(8,128)S(1)} reduce-window(s32[8,128]{1,0:T(8,128)} %bitcast.7, s32[]{:T(128)} %constant.3.clone.1), window={size=1x128 pad=0_0x127_0}, to_apply=%region_0.0 | reduce-window | flops 130048 | bytes 8196 | tf_op jit(solution)/shard_map/reduce-window
  2.8 0.1 slice.7
  2.9 0.1 slice_reduce_fusion
  3.0 0.1 reshape.38
  3.1 0.1 broadcast.16
  3.2 0.1 reshape.39
  3.3 1.3 %broadcast_in_dim.9.gain = bf16[1,1024]{1,0:T(2,128)(2,1)} reshape(bf16[1024]{0:T(1024)(128)(2,1)} %param.14) | data formatting | bytes 4096 | tf_op jit(solution)/shard_map/broadcast_in_dim | solution.py:294
  4.6 1.3 %broadcast_in_dim.10.out_gain = bf16[1,1024]{1,0:T(2,128)(2,1)} reshape(bf16[1024]{0:T(1024)(128)(2,1)} %param.19) | data formatting | bytes 4096 | tf_op jit(solution)/shard_map/broadcast_in_dim | solution.py:329
  5.8 0.1 reshape.37
  5.9 0.1 squeeze.7
  6.0 0.1 subtract_bitcast_fusion
  6.1 0.7 reshape.40.starts
  6.8 0.7 iota_add_fusion.positions
  7.5 69.2 %exchange.1 = (bf16[512,1024]{1,0:T(8,128)(2,1)}, bf16[1024,1024]{1,0:T(8,128)(2,1)}, bf16[1024,1024]{1,0:T(8,128)(2,1)}) custom-call(bf16[4,256,512]{2,1,0:T(8,128)(2,1)} %lat.1, bf16[4096,1024]{1,0:T(8,128)(2,1)} %wd.1, bf16[1,1024]{1,0:T(2,128)(2,1)} %broadcast_in_dim.9.gain, bf16[512,1024]{1,0:T(8,128)(2,1)} %bitcast.5, bf16[1024,1024]{1,0:T(8,128)(2,1)} %wq.1, ...), custom_call_target="tpu_custom_call" | custom-call | tf_op jit(solution)/shard_map/exchange/pallas_call | solution.py:264
  76.7 20.0 %attend.1 = bf16[512,1024]{1,0:T(8,128)(2,1)} custom-call(bf16[512,1024]{1,0:T(8,128)(2,1)} %get-tuple-element.8.q, bf16[1024,1024]{1,0:T(8,128)(2,1)} %get-tuple-element.9.k, bf16[1024,1024]{1,0:T(8,128)(2,1)} %get-tuple-element.10.v, s32[1,1024]{1,0:T(1,128)} %reshape.40.starts, s32[512,1]{1,0:T(8,128)} %iota_add_fusion.positions, ...), custom_call_target="tpu_custom_call" | custom-call | tf_op jit(solution)/shard_map/attend/pallas_call | solution.py:305
  (2 shorter events, 0.0 us)

commit v2 on v0

v2 whole, which is shorter than its diff:
```python
import functools

import jax
import jax.numpy as jnp
from jax import lax
from jax.experimental import pallas as pl
from jax.experimental.pallas import tpu as pltpu
from jax.sharding import PartitionSpec as P

HEADS = 16
HEAD_DIM = 64
MASKED = -1e30
MESH = pl.DeviceIdType.MESH


def rms_norm(values, gain_row):
    mean_square = jnp.mean(values * values, axis=-1, keepdims=True)
    return values * lax.rsqrt(mean_square + 1e-05) * gain_row


def layer_kernel(
    n_seq, n_mp, inner, parts,
    lat, wd, gain, bs, wq, wk, wv, wo, out_gain, lengths,
    out,
    latbuf, gbuf, acc, wd_v, bs_v, wq_v, wk_v, wv_v, wo_v,
    q_v, k_v, v_v, v_ext, starts_v, bias, num, den, peak, head_out,
    load_sem, send_sem, recv_sem, up_sem, down_sem, pair_sem, got_sem,
):
    my_s = lax.axis_index("seq")
    my_m = lax.axis_index("mp")
    total = n_seq * n_mp
    me = my_s * n_mp + my_m
    block = lat.shape[1] // parts
    piece = block // n_mp
    feats = lat.shape[2]
    tokens, width = bs_v.shape
    keys = k_v.shape[0]
    lanes = 2 * HEAD_DIM
    pairs = width // lanes
    rows = max(16, min(256, tokens, (256 * 512) // keys))
    blocks = tokens // rows
    tile = 256
    bf16, f32 = jnp.bfloat16, jnp.float32

    loads = [
        pltpu.make_async_copy(src, dst, load_sem.at[i])
        for i, (src, dst) in enumerate(
            [(bs, bs_v), (wq, wq_v), (wd, wd_v), (wk, wk_v), (wv, wv_v), (wo, wo_v)]
        )
    ]
    for load in loads:
        load.start()

    barrier = pltpu.get_barrier_semaphore()

    def greet(step, carry):
        other = lax.rem(me + step, total)
        pl.semaphore_signal(
            barrier, inc=1,
            device_id={"seq": other // n_mp, "mp": lax.rem(other, n_mp)},
            device_id_type=MESH,
        )
        return carry

    lax.fori_loop(1, total, greet, 0)
    pl.semaphore_wait(barrier, total - 1)

    def piece_of(h, t, m):
        return lat.at[t, pl.ds(pl.multiple_of(h * block + m * piece, piece), piece), :]

    def slot_of(h, s, m):
        return latbuf.at[h, m, pl.ds(pl.multiple_of(s * piece, piece), piece), :]

    def piece_copy(h, other):
        t, m = other // n_mp, lax.rem(other, n_mp)
        return pltpu.make_async_remote_copy(
            src_ref=piece_of(h, t, m),
            dst_ref=slot_of(h, my_s, my_m),
            send_sem=send_sem.at[h, other],
            recv_sem=recv_sem.at[h, me],
            device_id={"seq": t, "mp": m},
            device_id_type=MESH,
        )

    for h in range(parts):
        def send_piece(step, carry, h=h):
            piece_copy(h, lax.rem(me + step, total)).start()
            return carry

        lax.fori_loop(1, total, send_piece, 0)
        pltpu.make_async_copy(
            piece_of(h, my_s, my_m), slot_of(h, my_s, my_m), recv_sem.at[h, me]
        ).start()

    running = jnp.broadcast_to(lengths[...], (8, lengths.shape[1]))
    own_length = running
    lane_at = lax.broadcasted_iota(jnp.int32, running.shape, 1)
    shift = 1
    while shift < lengths.shape[1]:
        running = running + jnp.where(lane_at >= shift, pltpu.roll(running, shift, 1), 0)
        shift *= 2
    starts_v[...] = running - own_length
    v_ext[:, lanes:] = jnp.ones((keys, lanes), bf16)

    loads[0].wait()
    loads[1].wait()

    def query_tile(j, carry):
        cols = pl.ds(pl.multiple_of(j * tile, tile), tile)
        made = jnp.dot(bs_v[...], wq_v[:, cols], preferred_element_type=f32)
        q_v[:, cols] = made.astype(bf16) * bf16(HEAD_DIM**-0.5)
        return carry

    lax.fori_loop(0, width // tile, query_tile, 0)
    loads[2].wait()

    def project(h, first, last):
        def one(step, carry):
            m = lax.rem(my_m + step, n_mp)

            def arrived(s, inner_carry):
                here = slot_of(h, s, m)
                pltpu.make_async_copy(here, here, recv_sem.at[h, s * n_mp + m]).wait()
                return inner_carry

            lax.fori_loop(0, n_seq, arrived, 0)
            at = pl.ds(pl.multiple_of(m * feats, feats), feats)
            acc[...] += jnp.dot(latbuf[h, m], wd_v[at, :], preferred_element_type=f32)
            return carry

        if first == 0:
            acc[...] = jnp.zeros_like(acc)
        lax.fori_loop(first, last, one, 0)

    outer = n_mp // inner
    my_o = my_m // inner
    my_i = lax.rem(my_m, inner)
    partner = my_o * inner + (inner - 1 - my_i)
    has_up = my_o < outer - 1
    has_down = my_o > 0

    def row_copy(h, chunk, sem, target):
        return pltpu.make_async_remote_copy(
            src_ref=gbuf.at[h, :, chunk],
            dst_ref=gbuf.at[h, :, chunk],
            send_sem=sem.at[h, chunk],
            recv_sem=got_sem.at[h, chunk],
            device_id={"seq": my_s, "mp": target},
            device_id_type=MESH,
        )

    def wait_chunk(h, chunk):
        here = gbuf.at[h, :, chunk]
        pltpu.make_async_copy(here, here, got_sem.at[h, chunk]).wait()

    def go_up(h, chunk):
        return row_copy(h, chunk, up_sem, my_m + inner)

    def go_down(h, chunk):
        return row_copy(h, chunk, down_sem, my_m - inner)

    def go_pair(h, chunk):
        return row_copy(h, chunk, pair_sem, partner)

    def share(h):
        normed = rms_norm(acc[...], gain[...].astype(f32)[None, :]).astype(bf16)
        gbuf[h, :, my_m] = normed.reshape(n_seq, piece, width)
        pl.when(has_up)(lambda: go_up(h, my_m).start())
        pl.when(has_down)(lambda: go_down(h, my_m).start())
        go_pair(h, my_m).start()

    def relay(h, first, last):
        def one(k, carry):
            below = my_m - k * inner
            above = my_m + k * inner

            @pl.when(my_o - k >= 0)
            def _():
                wait_chunk(h, below)
                pl.when(has_up)(lambda: go_up(h, below).start())
                go_pair(h, below).start()

            @pl.when(my_o + k < outer)
            def _():
                wait_chunk(h, above)
                pl.when(has_down)(lambda: go_down(h, above).start())
                go_pair(h, above).start()

            return carry

        lax.fori_loop(first, last, one, 0)

    def take_pair(h):
        def one(o, carry):
            wait_chunk(h, o * inner + (inner - 1 - my_i))
            return carry

        lax.fori_loop(0, outer, one, 0)

    def keys_values(h):
        slab = min(keys, 512)

        def one(j, carry):
            cols = pl.ds(pl.multiple_of(j * tile, tile), tile)
            normed = gbuf[h].reshape(keys, width)
            for c in range(keys // slab):
                at = slice(c * slab, (c + 1) * slab)
                k_v[at, cols] = jnp.dot(
                    normed[at], wk_v[:, cols], preferred_element_type=f32
                ).astype(bf16)
                v_v[at, cols] = jnp.dot(
                    normed[at], wv_v[:, cols], preferred_element_type=f32
                ).astype(bf16)
            return carry

        lax.fori_loop(0, width // tile, one, 0)

    def mask(h):
        starts = jnp.concatenate(
            [
                starts_v[0:1, (s * parts + h) * block:(s * parts + h + 1) * block]
                for s in range(n_seq)
            ],
            axis=1,
        )
        position = my_m * tokens + lax.broadcasted_iota(jnp.int32, (tokens, 1), 0)
        bias[...] = jnp.where(starts <= position, 0.0, MASKED)

    low = lax.broadcasted_iota(jnp.int32, (rows, lanes), 1) < HEAD_DIM

    def attend(h, first, last):
        def one_pair(pair, carry):
            cols = pl.ds(pl.multiple_of(pair * lanes, lanes), lanes)
            v_ext[:, :lanes] = v_v[:, cols]

            def one_block(b, inner_carry):
                at = pl.ds(pl.multiple_of(b * rows, rows), rows)
                both = q_v[at, cols]
                made = []
                for half in range(2):
                    keep = low if half == 0 else ~low
                    q_half = jnp.where(keep, both, jnp.zeros_like(both))
                    scores = lax.dot_general(
                        q_half, k_v[:, cols], (((1,), (1,)), ((), ())),
                        preferred_element_type=f32,
                    ) + bias[at, :]
                    top = jnp.max(scores, axis=-1, keepdims=True)
                    weights = jnp.exp(scores - top).astype(bf16)
                    made.append(
                        (jnp.dot(weights, v_ext[...], preferred_element_type=f32), top)
                    )
                (sum0, top0), (sum1, top1) = made
                part = jnp.where(low, sum0[:, :lanes], sum1[:, :lanes])
                count = jnp.where(low, sum0[:, lanes:], sum1[:, lanes:])
                top = jnp.where(low, top0, top1)
                if h > 0:
                    before = peak[at, cols]
                    raised = jnp.maximum(before, top)
                    old, new = jnp.exp(before - raised), jnp.exp(top - raised)
                    part = num[at, cols] * old + part * new
                    count = den[at, cols] * old + count * new
                    top = raised
                if h == parts - 1:
                    head_out[at, cols] = (part / count).astype(bf16)
                else:
                    num[at, cols] = part
                    den[at, cols] = count
                    peak[at, cols] = top
                return inner_carry

            lax.fori_loop(0, blocks, one_block, 0, unroll=blocks <= 2)
            return carry

        lax.fori_loop(first, last, one_pair, 0)

    third = (outer + 1) // 3
    cut1, cut2 = min(1 + third, outer), min(1 + 2 * third, outer)
    project(0, 0, n_mp)
    share(0)
    relay(0, 1, cut1)
    project(1, 0, n_mp // 2)
    relay(0, cut1, cut2)
    project(1, n_mp // 2, n_mp)
    share(1)
    relay(0, cut2, outer)
    mask(0)
    loads[3].wait()
    loads[4].wait()
    loads[5].wait()
    relay(1, 1, cut1)
    take_pair(0)
    keys_values(0)
    relay(1, cut1, cut2)
    attend(0, 0, pairs // 2)
    relay(1, cut2, outer)
    attend(0, pairs // 2, pairs)
    mask(1)
    take_pair(1)
    keys_values(1)
    attend(1, 0, pairs)

    out_rows = min(tokens, 256)
    for r in range(tokens // out_rows):
        at = slice(r * out_rows, (r + 1) * out_rows)
        residual = bs_v[at, :].astype(f32) + jnp.dot(
            head_out[at, :], wo_v[...], preferred_element_type=f32
        )
        out[at, :] = rms_norm(residual, out_gain[...].astype(f32)[None, :]).astype(out.dtype)

    for h in range(parts):
        def finish_piece(step, carry, h=h):
            piece_copy(h, lax.rem(me + step, total)).wait_send()
            return carry

        lax.fori_loop(1, total, finish_piece, 0)

        def finish_rows(o, carry, h=h):
            chunk = o * inner + my_i
            pl.when(has_up & (o <= my_o))(lambda: go_up(h, chunk).wait_send())
            pl.when(has_down & (o >= my_o))(lambda: go_down(h, chunk).wait_send())
            go_pair(h, chunk).wait_send()
            return carry

        lax.fori_loop(0, outer, finish_rows, 0)


def per_device(n_seq, n_mp, byte_states, patch_latents, patch_lengths, w_down, kv_gain,
               w_query, w_key, w_value, w_out, out_gain):
    own_rows = byte_states[0]
    tokens, width = own_rows.shape
    patches = patch_lengths.shape[1]
    feats = patch_latents.shape[2]
    inner, parts = 2, 2
    here = patches // n_mp // parts
    keys = patches // parts
    any_spec = pl.BlockSpec(memory_space=pl.ANY)
    vmem_spec = pl.BlockSpec(memory_space=pltpu.VMEM)
    bf16, f32 = jnp.bfloat16, jnp.float32
    decoded = pl.pallas_call(
        functools.partial(layer_kernel, n_seq, n_mp, inner, parts),
        name="layer",
        out_shape=jax.ShapeDtypeStruct((tokens, width), bf16),
        in_specs=[any_spec, any_spec, vmem_spec] + [any_spec] * 5 + [vmem_spec] * 2,
        out_specs=vmem_spec,
        scratch_shapes=[
            pltpu.VMEM((parts, n_mp, here, feats), bf16),
            pltpu.VMEM((parts, n_seq, n_mp, here // n_seq, width), bf16),
            pltpu.VMEM((here, width), f32),
            pltpu.VMEM(w_down.shape, bf16),
            pltpu.VMEM((tokens, width), bf16),
            pltpu.VMEM(w_query.shape, bf16),
            pltpu.VMEM(w_key.shape, bf16),
            pltpu.VMEM(w_value.shape, bf16),
            pltpu.VMEM(w_out.shape, bf16),
            pltpu.VMEM((tokens, width), bf16),
            pltpu.VMEM((keys, width), bf16),
            pltpu.VMEM((keys, width), bf16),
            pltpu.VMEM((keys, 4 * HEAD_DIM), bf16),
            pltpu.VMEM((8, patches), jnp.int32),
            pltpu.VMEM((tokens, keys), f32),
            pltpu.VMEM((tokens, width), f32),
            pltpu.VMEM((tokens, width), f32),
            pltpu.VMEM((tokens, width), f32),
            pltpu.VMEM((tokens, width), bf16),
            pltpu.SemaphoreType.DMA((6,)),
            pltpu.SemaphoreType.DMA((parts, n_seq * n_mp)),
            pltpu.SemaphoreType.DMA((parts, n_seq * n_mp)),
            pltpu.SemaphoreType.DMA((parts, n_mp)),
            pltpu.SemaphoreType.DMA((parts, n_mp)),
            pltpu.SemaphoreType.DMA((parts, n_mp)),
            pltpu.SemaphoreType.DMA((parts, n_mp)),
        ],
        compiler_params=pltpu.CompilerParams(
            collective_id=0, has_side_effects=True, vmem_limit_bytes=63 * 1024 * 1024
        ),
    )(patch_latents, w_down, kv_gain, own_rows, w_query, w_key, w_value, w_out,
      out_gain, patch_lengths)
    return decoded[None]


def solution(mesh):
    return jax.shard_map(
        functools.partial(per_device, mesh.shape["seq"], mesh.shape["mp"]),
        mesh=mesh,
        in_specs=(
            P("seq", "mp", None),
            P(None, "seq", "mp"),
            P("seq", None),
            P(), P(), P(), P(), P(), P(), P(),
        ),
        out_specs=P("seq", "mp", None),
        check_vma=False,
    )
```

time: 286 us -> 80.8 us (0.28)
  the two profiles are of different devices: /device:TPU:16 before, /device:TPU:0 now
where the time goes in v2:
time: 80.8 us; the launch traced here: 80.6 us
  Pallas kernels  78.3 us (97%)
  local copies, waits for them, and re-layouts  2.26 us (3%)
    pallas_call x1, Pallas kernels, per_device(): pl.pallas_call(functools.partial(layer_kernel, n_seq, n_mp, inner, parts)...  78.3 us
    unnamed x1, local copies, waits for them, and re-layouts  2.26 us

profile of v2, /device:TPU:0, one launch (start us, length us, event | category | flops | bytes accessed | tf_op | source)
XLA Modules:
  0.0 80.6 jit_solution(8420911389879753661)
XLA Ops:
  0.0 78.3 %layer.1 = bf16[512,1024]{1,0:T(8,128)(2,1)} custom-call(bf16[4,256,512]{2,1,0:T(8,128)(2,1)} %lat.1, bf16[4096,1024]{1,0:T(8,128)(2,1)} %wd.1, bf16[1024]{0:T(1024)(128)(2,1)} %gain.1, bf16[512,1024]{1,0:T(8,128)(2,1)} %bitcast.3, bf16[1024,1024]{1,0:T(8,128)(2,1)} %wq.1, bf16[1024,1024]{1,0:T(8,128)(2,1)} %wk.1, bf16[1024,1024]{1,0:T(8,128)(2,1)} %wv.1, ...), custom_call_target="tpu_custom_call" | custom-call | tf_op jit(solution)/shard_map/layer/pallas_call | solution.py:339
  78.3 2.3 %copy.12 = bf16[1,512,1024]{2,1,0:T(8,128)(2,1)} copy(bf16[1,512,1024]{2,1,0:T(8,128)(2,1)} %bitcast.2) | data formatting | bytes 2097152

commit v3 on v2

--- a/solution.py
+++ b/solution.py
@@ -20,7 +20,7 @@
 
 def layer_kernel(
     n_seq, n_mp, inner, parts,
-    lat, wd, gain, bs, wq, wk, wv, wo, out_gain, lengths,
+    lat, wd, gain, bs, wq, wk, wv, wo, lengths,
     out,
     latbuf, gbuf, acc, wd_v, bs_v, wq_v, wk_v, wv_v, wo_v,
     q_v, k_v, v_v, v_ext, starts_v, bias, num, den, peak, head_out,
@@ -82,12 +82,16 @@
             device_id_type=MESH,
         )
 
+    def send_pieces(h, first, last):
+        def send_piece(step, carry):
+            piece_copy(h, lax.rem(me + step, total)).start()
+            return carry
+
+        lax.fori_loop(first, last, send_piece, 0)
+
     for h in range(parts):
-        def send_piece(step, carry, h=h):
-            piece_copy(h, lax.rem(me + step, total)).start()
-            return carry
-
-        lax.fori_loop(1, total, send_piece, 0)
+        send_pieces(h, 1, total)
+    for h in range(parts):
         pltpu.make_async_copy(
             piece_of(h, my_s, my_m), slot_of(h, my_s, my_m), recv_sem.at[h, me]
         ).start()
@@ -305,7 +309,8 @@
         residual = bs_v[at, :].astype(f32) + jnp.dot(
             head_out[at, :], wo_v[...], preferred_element_type=f32
         )
-        out[at, :] = rms_norm(residual, out_gain[...].astype(f32)[None, :]).astype(out.dtype)
+        mean_square = jnp.mean(residual * residual, axis=-1, keepdims=True)
+        out[at, :] = residual * lax.rsqrt(mean_square + 1e-05)
 
     for h in range(parts):
         def finish_piece(step, carry, h=h):
@@ -339,8 +344,8 @@
     decoded = pl.pallas_call(
         functools.partial(layer_kernel, n_seq, n_mp, inner, parts),
         name="layer",
-        out_shape=jax.ShapeDtypeStruct((tokens, width), bf16),
-        in_specs=[any_spec, any_spec, vmem_spec] + [any_spec] * 5 + [vmem_spec] * 2,
+        out_shape=jax.ShapeDtypeStruct((tokens, width), f32),
+        in_specs=[any_spec, any_spec, vmem_spec] + [any_spec] * 5 + [vmem_spec],
         out_specs=vmem_spec,
         scratch_shapes=[
             pltpu.VMEM((parts, n_mp, here, feats), bf16),
@@ -374,8 +379,8 @@
             collective_id=0, has_side_effects=True, vmem_limit_bytes=63 * 1024 * 1024
         ),
     )(patch_latents, w_down, kv_gain, own_rows, w_query, w_key, w_value, w_out,
-      out_gain, patch_lengths)
-    return decoded[None]
+      patch_lengths)
+    return (decoded * out_gain.astype(f32)).astype(bf16)[None]
 
 
 def solution(mesh):

time: 80.8 us -> 82.5 us (1.021)
  other arithmetic: 0 us -> 3.5 us
  local copies, waits for them, and re-layouts: 2.26 us -> 0 us
    broadcast_in_dim x0 -> x1, other arithmetic: none -> 2.82 us  [per_device(): return (decoded * out_gain.astype(f32)).astype(bf16)[None]]
    unnamed x1 -> x0, local copies, waits for them, and re-layouts: 2.26 us -> none
where the time goes in v3:
time: 82.5 us; the launch traced here: 82.2 us
  Pallas kernels  78.7 us (95%)
  other arithmetic  3.5 us (4%)
    pallas_call x1, Pallas kernels, per_device(): pl.pallas_call(functools.partial(layer_kernel, n_seq, n_mp, inner, parts)...  78.7 us
    broadcast_in_dim x1, other arithmetic, per_device(): return (decoded * out_gain.astype(f32)).astype(bf16)[None]  2.82 us

profile of v3, /device:TPU:0, one launch (start us, length us, event | category | flops | bytes accessed | tf_op | source)
XLA Modules:
  0.0 82.2 jit_solution(4603237156723180397)
XLA Ops:
  0.0 0.7 convert_element_type.6
  0.7 78.7 %layer.1 = f32[512,1024]{1,0:T(8,128)} custom-call(bf16[4,256,512]{2,1,0:T(8,128)(2,1)} %lat.1, bf16[4096,1024]{1,0:T(8,128)(2,1)} %wd.1, bf16[1024]{0:T(1024)(128)(2,1)} %gain.1, bf16[512,1024]{1,0:T(8,128)(2,1)} %bitcast.3, bf16[1024,1024]{1,0:T(8,128)(2,1)} %wq.1, bf16[1024,1024]{1,0:T(8,128)(2,1)} %wk.1, bf16[1024,1024]{1,0:T(8,128)(2,1)} %wv.1, ...), custom_call_target="tpu_custom_call" | custom-call | tf_op jit(solution)/shard_map/layer/pallas_call | solution.py:344
  79.4 2.8 %fusion = bf16[1,512,1024]{2,1,0:T(8,128)(2,1)} fusion(f32[512,1024]{1,0:T(8,128)} %layer.1, f32[1024]{0:T(1024)S(1)} %convert_element_type.6), kind=kLoop, calls=%fused_computation.1 | loop fusion | flops 1048576 | bytes 3149824 | tf_op jit(solution)/shard_map/broadcast_in_dim | solution.py:383
